TPU v7x, 32 devices: a whole 2x2x4 slice. The times are simulated.
32 devices in a mesh: gx: 4 (over x, core), gy: 8 (over z, y).
Axes of the slice: x: 2, y: 2, z: 4, core: 2. Of those that a mesh axis runs over, the one named last changes fastest.
Arguments:
- record_keys: int32 [32768], P(('gx', 'gy')), may hold values from 0 to 16777215
- payloads: int32 [32768], P(('gx', 'gy')), may hold values from 0 to 16777215
Outputs:
- sorted_keys: int32 [64512], P(('gx', 'gy'))
- sorted_payloads: int32 [64512], P(('gx', 'gy'))
- bucket_sizes: int32 [32], P(('gx', 'gy'))
- bucket_digest: int32 [32], P(('gx', 'gy'))
All inputs are finite; a program needn't handle non-finite values.
Results may differ from a plain program's by a relative error of at most 0.000001.
Values may be sent and summed in bfloat16 or wider, within the bound.
A program may use at most 64 MiB of HBM per device.

v0:
```python
import jax
import jax.numpy as jnp
from jax import lax
from jax.sharding import PartitionSpec as P

filler = 1073741824


def beneath_grid(run_keys, run_places, split_keys, split_places):
    return (run_keys[None, :] < split_keys[:, None]) | (
        run_keys[None, :] == split_keys[:, None]
    ) & (run_places[None, :] <= split_places[:, None])


def body(record_keys, payloads):
    devices = lax.axis_size(("gx", "gy"))
    per_device = record_keys.shape[0]
    spacing = per_device // devices
    bucket_cap = 2 * per_device - devices
    offset = lax.axis_index(("gx", "gy")) * per_device
    places = offset + lax.iota(jnp.int32, per_device)
    run_keys, run_places, run_values = lax.sort((record_keys, places, payloads), num_keys=2)
    sample_keys = run_keys.reshape(devices, spacing)[:, spacing - 1]
    sample_places = run_places.reshape(devices, spacing)[:, spacing - 1]
    every_keys, every_places = (
        lax.all_gather(sample_keys, ("gx", "gy"), axis=0, tiled=True),
        lax.all_gather(sample_places, ("gx", "gy"), axis=0, tiled=True),
    )
    every_keys, every_places = lax.sort((every_keys, every_places), num_keys=2)
    split_keys = every_keys.reshape(devices, devices)[: devices - 1, devices - 1]
    split_places = every_places.reshape(devices, devices)[: devices - 1, devices - 1]
    beneath = beneath_grid(run_keys, run_places, split_keys, split_places)
    bucket_of = devices - 1 - jnp.sum(beneath.astype(jnp.int32), axis=0)
    owners = lax.iota(jnp.int32, devices)
    mine = bucket_of[None, :] == owners[:, None]
    send_keys = jnp.where(mine, run_keys[None, :], filler)
    send_values = jnp.where(mine, run_values[None, :], filler)
    got_keys, got_values = (
        lax.all_to_all(send_keys, ("gx", "gy"), split_axis=0, concat_axis=0, tiled=True),
        lax.all_to_all(send_values, ("gx", "gy"), split_axis=0, concat_axis=0, tiled=True),
    )
    flat_keys, flat_values = lax.sort(
        (got_keys.reshape(-1), got_values.reshape(-1)), is_stable=True, num_keys=1
    )
    flat_keys = flat_keys[:bucket_cap]
    flat_values = flat_values[:bucket_cap]
    filled = flat_keys < filler
    sorted_keys = jnp.where(filled, flat_keys, -1)
    sorted_payloads = jnp.where(filled, flat_values, -1)
    bucket_size = jnp.sum(filled.astype(jnp.int32)).reshape(1)
    ranks = lax.iota(jnp.int32, bucket_cap)
    mixed = (sorted_keys + 3 * sorted_payloads + 5 * ranks) % 1024
    digest = jnp.sum(jnp.where(filled, 2 * mixed - 1023, 0)).astype(jnp.int32).reshape(1)
    return (sorted_keys, sorted_payloads, bucket_size, digest)


def solution(mesh):
    placed = (P(("gx", "gy")), P(("gx", "gy")))
    return jax.shard_map(
        body,
        mesh=mesh,
        in_specs=placed,
        out_specs=(P(("gx", "gy")), P(("gx", "gy")), P(("gx", "gy")), P(("gx", "gy"))),
        check_vma=False,
    )
```

profile of v0, /device:TPU:0, one launch (start us, length us, event | category | flops | bytes accessed | tf_op | source)
XLA Modules:
  0.0 94.7 jit_solution(370392090586647136)
XLA Ops:
  0.6 0.0 copy-start
  0.6 0.0 copy-start.1
  0.7 0.6 copy-done
  1.3 0.0 copy-done.1
  1.3 4.5 %sort.77 = (s32[1024]{0:T(1024)S(1)}, s32[1024]{0:T(1024)S(1)}, s32[1024]{0:T(1024)S(1)}, s32[1024]{0:T(1024)}) sort(s32[1024]{0:T(1024)S(1)} %copy-done, s32[1024]{0:T(1024)S(1)} %iota_add_fusion, s32[1024]{0:T(1024)S(1)} %copy-done.1, s32[1024]{0:T(1024)S(1)} %iota.25), dimensions={0}, to_apply=%region_0.0 | sort | flops 10240 | bytes 32768 | tf_op jit(solution)/shard_map/sort | solution.py:22
  5.9 0.1 reshape.132
  5.9 0.2 slice_reduce_fusion.2
  6.1 0.1 reshape.131
  6.2 0.2 slice_reduce_fusion.3
  6.4 0.2 dynamic-update-slice.1
  6.6 0.2 dynamic-update-slice
  6.8 42.0 %all-reduce.2 = (s32[1024]{0:T(1024)S(1)}, s32[1024]{0:T(1024)S(1)}) all-reduce(s32[1024]{0:T(1024)S(1)} %dynamic-update-slice, s32[1024]{0:T(1024)S(1)} %dynamic-update-slice.1), channel_id=2, replica_groups=mesh['gx'=4,'gy'=8] {'gx','gy'}, use_global_device_ids=true, to_apply=%add | all-reduce | flops 2048 | bytes 16384 | tf_op jit(solution)/shard_map/all_gather | solution.py:26
  48.9 4.5 %sort.78 = (s32[1024]{0:T(1024)S(1)}, s32[1024]{0:T(1024)S(1)}, s32[1024]{0:T(1024)}) sort(s32[1024]{0:T(1024)S(1)} %get-tuple-element.27, s32[1024]{0:T(1024)S(1)} %get-tuple-element.28, s32[1024]{0:T(1024)S(1)} %iota.26), dimensions={0}, to_apply=%region_1.0 | sort | flops 10240 | bytes 24576 | tf_op jit(solution)/shard_map/sort | solution.py:29
  53.3 0.1 reshape.133
  53.4 0.1 reshape.134
  53.5 0.2 slice_reduce_fusion
  53.7 0.1 convert_reduce_fusion
  53.8 0.2 compare_select_fusion
  54.0 12.1 %all_to_all.12 = s32[32,1,1024]{2,1,0:T(1,128)S(1)} all-to-all(s32[32,1,1024]{2,1,0:T(1,128)S(1)} %get-tuple-element.31), channel_id=1, replica_groups=mesh['gx'=4,'gy'=8] {'gx','gy'}, dimensions={0} | all-to-all | bytes 262144 | tf_op jit(solution)/shard_map/all_to_all | solution.py:40
  66.1 10.0 %all_to_all.13 = s32[32,1,1024]{2,1,0:T(1,128)S(1)} all-to-all(s32[32,1,1024]{2,1,0:T(1,128)S(1)} %get-tuple-element.32), channel_id=1, replica_groups=mesh['gx'=4,'gy'=8] {'gx','gy'}, dimensions={0} | all-to-all | bytes 262144 | tf_op jit(solution)/shard_map/all_to_all | solution.py:39
  76.1 17.4 %sort.79 = (s32[32768]{0:T(1024)S(1)}, s32[32768]{0:T(1024)S(1)}, s32[32768]{0:T(1024)}) sort(s32[32768]{0:T(1024)S(1)} %bitcast.5, s32[32768]{0:T(1024)S(1)} %bitcast.4, s32[32768]{0:T(1024)S(1)} %iota.27), dimensions={0}, to_apply=%region_3.4 | sort | flops 491520 | bytes 786432 | tf_op jit(solution)/shard_map/sort | solution.py:42
  93.5 1.2 %fusion.4 = (s32[]{:T(128)}, s32[]{:T(128)}, s32[2016]{0:T(1024)}, s32[2016]{0:T(1024)}) fusion(s32[32768]{0:T(1024)S(1)} %get-tuple-element.24, s32[32768]{0:T(1024)S(1)} %get-tuple-element.23), kind=kLoop, calls=%fused_computation.14 | loop fusion | flops 48382 | bytes 32264 | tf_op jit(solution)/shard_map/reduce_sum | solution.py:53
  (7 shorter events, 0.0 us)
Async XLA Ops:
  0.6 0.7 copy-start
  0.6 0.7 copy-start.1
where the time goes:
time: 95.1 us; the launch traced here: 94.7 us
  blocking collectives  64.1 us (67%)
  other arithmetic  27.9 us (29%)
  local copies, waits for them, and re-layouts  1.97 us (2%)
    all_gather x1, blocking collectives, body(): lax.all_gather(sample_keys, ('gx', 'gy'), axis=0, tiled=True)  42 us
    sort x1, other arithmetic, body(): lax.sort((got_keys.reshape(-1), got_values.reshape(-1)), is_stable=True,...  17.4 us
    all_to_all x1, blocking collectives, body(): lax.all_to_all(send_values, ('gx', 'gy'), split_axis=0, concat_axis=0, ti...  12.1 us
    all_to_all x1, blocking collectives, body(): lax.all_to_all(send_keys, ('gx', 'gy'), split_axis=0, concat_axis=0, tile...  9.96 us
    sort x1, other arithmetic, body(): lax.sort((record_keys, places, payloads), num_keys=2)  4.52 us
    sort x1, other arithmetic, body(): every_keys, every_places = lax.sort((every_keys, every_places), num_keys=2)  4.48 us

commit v1 on v0

v1 whole, which is shorter than its diff:
```python
import functools

import jax
import jax.numpy as jnp
from jax import lax
from jax.experimental import pallas as pl
from jax.experimental.pallas import tpu as pltpu
from jax.sharding import PartitionSpec as P

MESH = pl.DeviceIdType.MESH
LANES = 128
filler = 1073741824


def rank_rows(keys, rows):
    counts = [jnp.zeros((8, LANES), jnp.int32) for _ in range(rows)]
    turned = keys.T
    sub = lax.broadcasted_iota(jnp.int32, (LANES, LANES), 0)
    lane = lax.broadcasted_iota(jnp.int32, (LANES, LANES), 1)
    earlier = (sub < lane).astype(jnp.int32)
    for c in range(rows):
        column = jnp.broadcast_to(turned[:, c : c + 1], (LANES, LANES))
        for b in range(rows):
            row = keys[b : b + 1, :]
            if c < b:
                below = column <= row
            elif c > b:
                below = column < row
            else:
                below = column < row + earlier
            counts[b] = counts[b] + jnp.sum(below.astype(jnp.int32).reshape(LANES // 8, 8, LANES), axis=0)
    return [jnp.sum(count, axis=0, keepdims=True) for count in counts]


def place_rows(ranks, keys, values, rows, left_ref, right_ref):
    sub = lax.broadcasted_iota(jnp.int32, (LANES, LANES), 0)
    high = lax.broadcasted_iota(jnp.int32, (rows, LANES), 0)
    for b in range(rows):
        rank = ranks[b]
        at = slice(b * LANES, (b + 1) * LANES)
        right_ref[:, at] = (sub == (rank & (LANES - 1))).astype(jnp.float32).astype(jnp.bfloat16)
        mine = high == (rank >> 7)
        pieces = []
        for array in (keys, values):
            row = array[b : b + 1, :]
            for shift in (0, 8, 16):
                byte = ((row >> shift) & 255).astype(jnp.float32)
                pieces.append(jnp.where(mine, byte, 0.0))
        left_ref[:, at] = jnp.concatenate(pieces, axis=0).astype(jnp.bfloat16)
    moved = lax.dot_general(
        left_ref[...], right_ref[...], (((1,), (1,)), ((), ())), preferred_element_type=jnp.float32
    )
    part = [moved[i * rows : (i + 1) * rows, :] for i in range(6)]
    key = part[0] + 256.0 * part[1] + 65536.0 * part[2]
    value = part[3] + 256.0 * part[4] + 65536.0 * part[5]
    return key.astype(jnp.int32), value.astype(jnp.int32)


def local_kernel(rows, key_ref, value_ref, run_ref, left_ref, right_ref):
    keys, values = key_ref[...], value_ref[...]
    ranks = rank_rows(keys, rows)
    key, value = place_rows(ranks, keys, values, rows, left_ref, right_ref)
    run_ref[:rows, :] = key
    run_ref[rows:, :] = value


def gather_kernel(devices, inner, run_ref, all_ref, send_sem, recv_sem):
    me = lax.axis_index(("gx", "gy"))

    def place(other):
        return (other // inner, lax.rem(other, inner))

    barrier = pltpu.get_barrier_semaphore()

    @pl.loop(1, devices)
    def _(k):
        pl.semaphore_signal(barrier, inc=1, device_id=place(lax.rem(me + k, devices)), device_id_type=MESH)

    pl.semaphore_wait(barrier, devices - 1)

    def copy(k, owner):
        return pltpu.make_async_remote_copy(
            src_ref=run_ref,
            dst_ref=all_ref.at[owner],
            send_sem=send_sem.at[k],
            recv_sem=recv_sem.at[owner],
            device_id=place(lax.rem(me + k, devices)),
            device_id_type=MESH,
        )

    @pl.loop(1, devices)
    def _(k):
        copy(k, me).start()

    all_ref[me] = run_ref[...]

    @pl.loop(1, devices)
    def _(k):
        copy(k, lax.rem(me + devices - k, devices)).wait_recv()

    @pl.loop(1, devices)
    def _(k):
        copy(k, me).wait_send()


def bucket_kernel(devices, rows, low_ref, start_ref, stop_ref, all_ref, key_ref, value_ref, digest_ref, left_ref, right_ref):
    span = rows * LANES
    lane = lax.broadcasted_iota(jnp.int32, (rows, LANES), 1)
    spot = lax.broadcasted_iota(jnp.int32, (rows, LANES), 0) * LANES + lane

    def take(r, held):
        k0, k1, v0, v1 = held
        start, stop = start_ref[r], stop_ref[r]
        turn = (start - low_ref[r]) & (span - 1)
        across, down = turn & (LANES - 1), turn >> 7

        def rotate(x):
            x = pltpu.roll(x, across, 1)
            return jnp.where(lane < across, pltpu.roll(x, (down + 1) & (rows - 1), 0), pltpu.roll(x, down, 0))

        k, v = rotate(all_ref[r, :rows, :]), rotate(all_ref[r, rows:, :])
        first = (spot >= start) & (spot < stop)
        second = (spot + span >= start) & (spot + span < stop)
        return (
            jnp.where(first, k, k0),
            jnp.where(second, k, k1),
            jnp.where(first, v, v0),
            jnp.where(second, v, v1),
        )

    empty = jnp.full((rows, LANES), filler, jnp.int32)
    none = jnp.zeros((rows, LANES), jnp.int32)
    k0, k1, v0, v1 = lax.fori_loop(0, devices, take, (empty, empty, none, none), unroll=8)
    keys, values = jnp.concatenate([k0, k1], axis=0), jnp.concatenate([v0, v1], axis=0)
    ranks = rank_rows(keys, 2 * rows)
    key, value = place_rows(ranks, keys, values, 2 * rows, left_ref, right_ref)
    rank = lax.broadcasted_iota(jnp.int32, (2 * rows, LANES), 0) * LANES + lax.broadcasted_iota(
        jnp.int32, (2 * rows, LANES), 1
    )
    filled = rank < stop_ref[devices - 1]
    key_ref[...] = jnp.where(filled, key, -1)
    value_ref[...] = jnp.where(filled, value, -1)
    mixed = (key + 3 * value + 5 * rank) & 1023
    digest_ref[0] = jnp.sum(jnp.where(filled, 2 * mixed - 1023, 0))


def body(inner, record_keys, payloads):
    devices = lax.axis_size(("gx", "gy"))
    per_device = record_keys.shape[0]
    spacing = per_device // devices
    bucket_cap = 2 * per_device - devices
    rows = per_device // LANES
    me = lax.axis_index(("gx", "gy"))
    vmem = pl.BlockSpec(memory_space=pltpu.VMEM)
    smem = pl.BlockSpec(memory_space=pltpu.SMEM)
    run = pl.pallas_call(
        functools.partial(local_kernel, rows),
        out_shape=jax.ShapeDtypeStruct((2 * rows, LANES), jnp.int32),
        in_specs=[vmem] * 2,
        out_specs=vmem,
        scratch_shapes=[
            pltpu.VMEM((6 * rows, per_device), jnp.bfloat16),
            pltpu.VMEM((LANES, per_device), jnp.bfloat16),
        ],
    )(record_keys.reshape(rows, LANES), payloads.reshape(rows, LANES))
    runs = pl.pallas_call(
        functools.partial(gather_kernel, devices, inner),
        out_shape=jax.ShapeDtypeStruct((devices, 2 * rows, LANES), jnp.int32),
        in_specs=[vmem],
        out_specs=vmem,
        scratch_shapes=[pltpu.SemaphoreType.DMA((devices,)), pltpu.SemaphoreType.DMA((devices,))],
        compiler_params=pltpu.CompilerParams(collective_id=0, has_side_effects=True),
    )(run)
    run_keys = runs[:, :rows, :].reshape(devices, per_device)
    samples = run_keys.reshape(devices, devices, spacing)[:, :, spacing - 1].reshape(-1)
    order = lax.iota(jnp.int32, devices * devices)
    beneath = samples[:, None] < samples[None, :] + (order[:, None] < order[None, :]).astype(jnp.int32)
    ranks = jnp.sum(beneath.astype(jnp.int32), axis=0)
    index = lax.iota(jnp.int32, per_device)[None, :]
    run_of = lax.iota(jnp.int32, devices)[:, None]

    def reach(j):
        chosen = ranks == j * devices - 1
        key = jnp.sum(jnp.where(chosen, samples, 0))
        which = jnp.sum(jnp.where(chosen, order, 0))
        sample_run, sample_index = which // devices, (which % devices) * spacing + spacing - 1
        ahead = (run_of < sample_run) | (run_of == sample_run) & (index <= sample_index)
        count = jnp.sum((run_keys < key + ahead.astype(jnp.int32)).astype(jnp.int32), axis=1)
        return jnp.where(j == 0, 0, jnp.where(j == devices, per_device, count))

    low, high = reach(me), reach(me + 1)
    each = lax.iota(jnp.int32, devices)
    stop = jnp.sum(jnp.where(each[:, None] <= each[None, :], (high - low)[:, None], 0), axis=0)
    start = stop - (high - low)
    sorted_keys, sorted_payloads, digest = pl.pallas_call(
        functools.partial(bucket_kernel, devices, rows),
        out_shape=(
            jax.ShapeDtypeStruct((2 * rows, LANES), jnp.int32),
            jax.ShapeDtypeStruct((2 * rows, LANES), jnp.int32),
            jax.ShapeDtypeStruct((1,), jnp.int32),
        ),
        in_specs=[smem] * 3 + [vmem],
        out_specs=(vmem, vmem, smem),
        scratch_shapes=[
            pltpu.VMEM((12 * rows, 2 * per_device), jnp.bfloat16),
            pltpu.VMEM((LANES, 2 * per_device), jnp.bfloat16),
        ],
    )(low, start, stop, runs)
    size = stop[devices - 1].reshape(1)
    return (sorted_keys.reshape(-1)[:bucket_cap], sorted_payloads.reshape(-1)[:bucket_cap], size, digest)


def solution(mesh):
    placed = P(("gx", "gy"))
    return jax.shard_map(
        functools.partial(body, mesh.shape["gy"]),
        mesh=mesh,
        in_specs=(placed, placed),
        out_specs=(placed,) * 4,
        check_vma=False,
    )
```

time: 95.1 us -> 37.6 us (0.40)
  blocking collectives: 64.1 us -> 0 us
  Pallas kernels: 0 us -> 22.5 us
  other arithmetic: 27.9 us -> 5.67 us
  between operations: 0.72 us -> 5.97 us
  local copies, waits for them, and re-layouts: 1.97 us -> 3.05 us
    all_gather x1 -> x0, blocking collectives: 42 us -> none  [body(): lax.all_gather(sample_keys, ('gx', 'gy'), axis=0, tiled=True)]
    sort x3 -> x0, other arithmetic: 26.4 us -> none  [the longest x1 17.4 us: body(): lax.sort((got_keys.reshape(-1), got_values.reshape(-1)), is_stable=True,...]
    pallas_call x0 -> x3, Pallas kernels: none -> 22.5 us  [the longest x1 16.1 us: body(): pl.pallas_call(functools.partial(gather_kernel, devices, inner), out_shap...]
    all_to_all x2 -> x0, blocking collectives: 22.1 us -> none  [the longest x1 12.1 us: body(): lax.all_to_all(send_values, ('gx', 'gy'), split_axis=0, concat_axis=0, ti...]
    reduce_sum x2 -> x5, other arithmetic: 1.35 us -> 4.59 us  [the longest x1 2.66 us: reach(): jnp.sum((run_keys < key + ahead.astype(jnp.int32)).astype(jnp.int32), axi...]
    slice x3, local copies, waits for them, and re-layouts: 0.55 us -> 2.36 us  [the longest x1 1.25 us: body(): size = stop[devices - 1].reshape(1)]
    sub x1 -> x2, other arithmetic: 0.01 us -> 1.06 us  [the longest x1 0.54 us: body(): start = stop - (high - low)]
where the time goes in v1:
time: 37.6 us; the launch traced here: 37.2 us
  Pallas kernels  22.5 us (60%)
  between operations  5.97 us (16%)
  other arithmetic  5.67 us (15%)
  local copies, waits for them, and re-layouts  3.05 us (8%)
    pallas_call x1, Pallas kernels, body(): pl.pallas_call(functools.partial(gather_kernel, devices, inner), out_shap...  16.1 us
    pallas_call x1, Pallas kernels, body(): pl.pallas_call(functools.partial(bucket_kernel, devices, rows), out_shape...  4.28 us
    reduce_sum x1, other arithmetic, reach(): jnp.sum((run_keys < key + ahead.astype(jnp.int32)).astype(jnp.int32), axi...  2.66 us
    pallas_call x1, Pallas kernels, body(): pl.pallas_call(functools.partial(local_kernel, rows), out_shape=jax.Shape...  2.14 us
    slice x1, local copies, waits for them, and re-layouts, body(): size = stop[devices - 1].reshape(1)  1.25 us
    slice x1, local copies, waits for them, and re-layouts, body(): run_keys = runs[:, :rows, :].reshape(devices, per_device)  0.91 us

profile of v1, /device:TPU:0, one launch (start us, length us, event | category | flops | bytes accessed | tf_op | source)
XLA Modules:
  0.0 37.2 jit_solution(15654376067369503878)
XLA Ops:
  0.6 2.1 %shard_map.57.run_ref = s32[16,128]{1,0:T(8,128)} custom-call(s32[8,128]{1,0:T(8,128)} %bitcast.8, s32[8,128]{1,0:T(8,128)} %bitcast.9), custom_call_target="tpu_custom_call" | custom-call | tf_op jit(solution)/shard_map/pallas_call | solution.py:156
  2.8 16.1 %shard_map.58.all_ref = s32[32,16,128]{2,1,0:T(8,128)} custom-call(s32[16,128]{1,0:T(8,128)} %shard_map.57.run_ref), custom_call_target="tpu_custom_call" | custom-call | tf_op jit(solution)/shard_map/pallas_call | solution.py:166
  18.9 0.9 %slice.15 = s32[32,8,128]{2,1,0:T(8,128)S(1)} slice(s32[32,16,128]{2,1,0:T(8,128)} %shard_map.58.all_ref), slice={[0:32], [0:8], [0:128]} | slice | bytes 262144 | tf_op jit(solution)/shard_map/slice | solution.py:174
  19.8 0.2 reshape_reshape.3
  20.0 0.2 slice.20
  20.2 0.0 copy-start
  20.2 0.2 copy.8
  20.5 0.1 lt.63
  20.5 0.6 %convert_reduce_fusion = s32[1024]{0:T(1024)S(1)} fusion(s32[1024]{0:T(1024)S(1)} %lt.63), kind=kLoop, calls=%fused_computation | loop fusion | flops 6290432 | bytes 8192 | tf_op jit(solution)/shard_map/reduce_sum | solution.py:178
  21.1 0.6 %select_reduce_fusion.4 = (s32[]{:T(128)}, pred[1024]{0:T(1024)(128)(4,1)S(1)}, s32[]{:T(128)}, pred[1024]{0:T(1024)(128)(4,1)S(1)}) fusion(s32[1024]{0:T(1024)S(1)} %convert_reduce_fusion, s32[]{:T(128)S(6)} %sub.30, s32[]{:T(128)S(6)} %sub.33), kind=kLoop, calls=%fused_computation.15 | loop fusion | flops 6142 | bytes 6160 | tf_op jit(solution)/shard_map/reduce_sum | solution.py:185
  21.7 0.1 eq.75
  21.8 0.1 eq.69
  21.9 0.6 %select_reduce_fusion.1 = (s32[]{:T(128)}, s32[]{:T(128)}) fusion(pred[32,32,1]{1,0,2:T(8,128)(4,1)S(1)} %eq.75, s32[32,32,1]{1,0,2:T(8,128)S(1)} %copy.8, pred[32,32,1]{1,0,2:T(8,128)(4,1)S(1)} %eq.69), kind=kLoop, calls=%fused_computation.8 | loop fusion | flops 4094 | bytes 6152 | tf_op jit(solution)/shard_map/reduce_sum | solution.py:184
  27.8 0.0 copy-done
  27.8 2.7 %convert_reduce_fusion.1 = (s32[32]{0:T(128)S(1)}, s32[32]{0:T(128)S(1)}) fusion(s32[]{:T(128)} %get-tuple-element.12, pred[32]{0:T(512)(128)(4,1)S(1)} %get-tuple-element.23, pred[8,128]{1,0:T(8,128)(4,1)S(1)} %get-tuple-element.26, pred[32]{0:T(512)(128)(4,1)S(1)} %get-tuple-element.22, s32[32,16,128]{2,1,0:T(8,128)S(1)} %copy-done, ...), kind=kLoop, calls=%fused_computation.3 | loop fusion | flops 458688 | bytes 133512 | tf_op jit(solution)/shard_map/reduce_sum | solution.py:188
  30.5 0.5 %fusion.2 = (s32[32]{0:T(128)S(1)}, s32[32]{0:T(128)}) fusion(pred[]{:T(512)S(6)} %eq.71, s32[32]{0:T(128)S(1)} %get-tuple-element.10, pred[]{:T(512)S(6)} %eq.72, s32[32]{0:T(128)S(1)} %get-tuple-element.11, pred[]{:T(512)S(6)} %eq.66, pred[]{:T(512)S(6)} %eq.65), kind=kLoop, calls=%fused_computation.22 | loop fusion | flops 160 | bytes 516 | tf_op jit(solution)/shard_map/sub | solution.py:193
  31.0 0.1 select_reduce_fusion.stop_ref
  31.1 0.0 copy-start.1
  31.1 0.5 %sub.37.start_ref = s32[32]{0:T(128)} subtract(s32[32]{0:T(128)S(1)} %select_reduce_fusion.stop_ref, s32[32]{0:T(128)S(1)} %get-tuple-element.14) | non-fusion elementwise | flops 32 | bytes 384 | tf_op jit(solution)/shard_map/sub | solution.py:194
  31.7 0.0 copy-done.1
  31.7 4.3 %shard_map.59 = (s32[16,128]{1,0:T(8,128)}, s32[16,128]{1,0:T(8,128)}, s32[1]{0:T(128)}) custom-call(s32[32]{0:T(128)} %get-tuple-element.15.low_ref, s32[32]{0:T(128)} %sub.37.start_ref, s32[32]{0:T(128)} %copy-done.1, s32[32,16,128]{2,1,0:T(8,128)} %shard_map.58.all_ref), custom_call_target="tpu_custom_call" | custom-call | tf_op jit(solution)/shard_map/pallas_call | solution.py:195
  36.0 1.2 %slice.19 = s32[1]{0:T(128)} slice(s32[32]{0:T(128)} %copy-done.1), slice={[31:32]} | slice | bytes 8 | tf_op jit(solution)/shard_map/slice | solution.py:209
  (3 shorter events, 0.0 us)
Async XLA Ops:
  20.2 7.6 %copy-start = (s32[32,16,128]{2,1,0:T(8,128)S(1)}, s32[32,16,128]{2,1,0:T(8,128)}, u32[]{:S(2)}) copy-start(s32[32,16,128]{2,1,0:T(8,128)} %shard_map.58.all_ref) | copy-start | bytes 786436
  31.1 0.6 %copy-start.1 = (s32[32]{0:T(128)}, s32[32]{0:T(128)S(1)}, u32[]{:S(2)}) copy-start(s32[32]{0:T(128)S(1)} %select_reduce_fusion.stop_ref) | copy-start | bytes 388

commit v2 on v1

--- a/solution.py
+++ b/solution.py
@@ -103,20 +103,111 @@
         copy(k, me).wait_send()
 
 
-def bucket_kernel(devices, rows, low_ref, start_ref, stop_ref, all_ref, key_ref, value_ref, digest_ref, left_ref, right_ref):
+def dot(left, right):
+    return jnp.dot(
+        left.astype(jnp.float32).astype(jnp.bfloat16),
+        right.astype(jnp.float32).astype(jnp.bfloat16),
+        preferred_element_type=jnp.float32,
+    )
+
+
+def splitter_pair(devices, spacing, me, keys, turned_ref, keys_ref, count_ref):
+    height = keys.shape[0]
+    blocks = height // LANES
+    many = LANES // spacing
+    keys_ref[...] = keys
+    for b in range(blocks):
+        turned = keys[b * LANES : (b + 1) * LANES, :].T
+        turned_ref[b] = jnp.concatenate([turned[i * spacing + spacing - 1 :][:1, :] for i in range(many)], axis=0)
+    count_ref[...] = jnp.zeros_like(count_ref)
+    sub = lax.broadcasted_iota(jnp.int32, (LANES, LANES), 0)
+    lane = lax.broadcasted_iota(jnp.int32, (LANES, LANES), 1)
+
+    def pair(c, b):
+        strict = (sub + c * LANES < lane + b * LANES).astype(jnp.int32)
+        loose = (sub + c * LANES <= lane + b * LANES).astype(jnp.int32)
+        row_block = turned_ref[b]
+        column_block = keys_ref[pl.ds(c * LANES, LANES), :]
+        columns = []
+        for j in range(many):
+            at = j * spacing + spacing - 1
+            columns.append(jnp.broadcast_to(column_block[:, at : at + 1], (LANES, LANES)))
+        for i in range(many):
+            row = jnp.broadcast_to(row_block[i : i + 1, :], (LANES, LANES))
+            row_strict, row_loose = row + strict, row + loose
+            total = jnp.zeros((8, LANES), jnp.int32)
+            for j in range(many):
+                below = columns[j] < (row_loose if j < i else row_strict)
+                total = total + jnp.sum(below.astype(jnp.int32).reshape(LANES // 8, 8, LANES), axis=0)
+            count_ref[b * many + i] += total
+
+    if blocks <= 2:
+        for c in range(blocks):
+            for b in range(blocks):
+                pair(c, b)
+    else:
+
+        @pl.loop(0, blocks)
+        def _(c):
+            @pl.loop(0, blocks)
+            def _(b):
+                pair(c, b)
+
+    ranks = jnp.sum(count_ref[...], axis=1)
+    samples = turned_ref[...].reshape(blocks * many, LANES)
+    line = lax.broadcasted_iota(jnp.int32, (blocks * many, LANES), 0)
+    across = lax.broadcasted_iota(jnp.int32, (blocks * many, LANES), 1)
+    block = line // many
+    flat = (block * LANES + across) * LANES + (line - block * many) * spacing + spacing - 1
+
+    def pick(j):
+        chosen = ranks == j * devices - 1
+        key = jnp.sum(jnp.where(chosen, samples, 0), axis=(0, 1), keepdims=True)
+        place = jnp.sum(jnp.where(chosen, flat, 0), axis=(0, 1), keepdims=True)
+        key = jnp.where(j == 0, -1, jnp.where(j == devices, filler, key))
+        return key, place
+
+    return pick(me), pick(me + 1)
+
+
+def bucket_kernel(
+    devices, rows, spacing, all_ref, key_ref, value_ref, size_ref, digest_ref,
+    left_ref, right_ref, turned_ref, keys_ref, count_ref, lows_ref, starts_ref, stops_ref,
+):
+    me = lax.axis_index(("gx", "gy"))
     span = rows * LANES
+    height = devices * rows
     lane = lax.broadcasted_iota(jnp.int32, (rows, LANES), 1)
-    spot = lax.broadcasted_iota(jnp.int32, (rows, LANES), 0) * LANES + lane
+    sub = lax.broadcasted_iota(jnp.int32, (rows, LANES), 0)
+    spot = sub * LANES + lane
+
+    keys = all_ref[:, :rows, :].reshape(height, LANES)
+    low, high = splitter_pair(devices, spacing, me, keys, turned_ref, keys_ref, count_ref)
+    flat = lax.broadcasted_iota(jnp.int32, (height, LANES), 0) * LANES + lax.broadcasted_iota(
+        jnp.int32, (height, LANES), 1
+    )
+    ones = jnp.ones((LANES, LANES), jnp.int32)
+    below_low = dot((keys < low[0] + (flat <= low[1]).astype(jnp.int32)).astype(jnp.int32), ones)
+    below_high = dot((keys < high[0] + (flat <= high[1]).astype(jnp.int32)).astype(jnp.int32), ones)
+    run = lax.broadcasted_iota(jnp.int32, (devices, height), 0)
+    run_of = lax.broadcasted_iota(jnp.int32, (devices, height), 1) // rows
+    inside = below_high - below_low
+    lows_ref[...] = dot((run_of == run).astype(jnp.int32), below_low).astype(jnp.int32)
+    starts_ref[...] = dot((run_of < run).astype(jnp.int32), inside).astype(jnp.int32)
+    stops_ref[...] = dot((run_of <= run).astype(jnp.int32), inside).astype(jnp.int32)
 
     def take(r, held):
         k0, k1, v0, v1 = held
-        start, stop = start_ref[r], stop_ref[r]
-        turn = (start - low_ref[r]) & (span - 1)
+        start = jnp.broadcast_to(starts_ref[pl.ds(r, 1), :], (rows, LANES))
+        stop = jnp.broadcast_to(stops_ref[pl.ds(r, 1), :], (rows, LANES))
+        turn = (start - lows_ref[pl.ds(r, 1), :]) & (span - 1)
         across, down = turn & (LANES - 1), turn >> 7
+        from_lane = (lane - across) & (LANES - 1)
+        from_row = (sub - down - (lane < across).astype(jnp.int32)) & (rows - 1)
 
         def rotate(x):
-            x = pltpu.roll(x, across, 1)
-            return jnp.where(lane < across, pltpu.roll(x, (down + 1) & (rows - 1), 0), pltpu.roll(x, down, 0))
+            x = jnp.take_along_axis(x, from_lane, axis=1)
+            return jnp.take_along_axis(x, from_row, axis=0)
 
         k, v = rotate(all_ref[r, :rows, :]), rotate(all_ref[r, rows:, :])
         first = (spot >= start) & (spot < stop)
@@ -131,17 +222,19 @@
     empty = jnp.full((rows, LANES), filler, jnp.int32)
     none = jnp.zeros((rows, LANES), jnp.int32)
     k0, k1, v0, v1 = lax.fori_loop(0, devices, take, (empty, empty, none, none), unroll=8)
-    keys, values = jnp.concatenate([k0, k1], axis=0), jnp.concatenate([v0, v1], axis=0)
-    ranks = rank_rows(keys, 2 * rows)
-    key, value = place_rows(ranks, keys, values, 2 * rows, left_ref, right_ref)
+    held_keys, held_values = jnp.concatenate([k0, k1], axis=0), jnp.concatenate([v0, v1], axis=0)
+    ranks = rank_rows(held_keys, 2 * rows)
+    key, value = place_rows(ranks, held_keys, held_values, 2 * rows, left_ref, right_ref)
     rank = lax.broadcasted_iota(jnp.int32, (2 * rows, LANES), 0) * LANES + lax.broadcasted_iota(
         jnp.int32, (2 * rows, LANES), 1
     )
-    filled = rank < stop_ref[devices - 1]
+    size = stops_ref[devices - 1 :, :]
+    filled = rank < size
     key_ref[...] = jnp.where(filled, key, -1)
     value_ref[...] = jnp.where(filled, value, -1)
     mixed = (key + 3 * value + 5 * rank) & 1023
     digest_ref[0] = jnp.sum(jnp.where(filled, 2 * mixed - 1023, 0))
+    size_ref[0] = jnp.max(size)
 
 
 def body(inner, record_keys, payloads):
@@ -150,7 +243,6 @@
     spacing = per_device // devices
     bucket_cap = 2 * per_device - devices
     rows = per_device // LANES
-    me = lax.axis_index(("gx", "gy"))
     vmem = pl.BlockSpec(memory_space=pltpu.VMEM)
     smem = pl.BlockSpec(memory_space=pltpu.SMEM)
     run = pl.pallas_call(
@@ -171,42 +263,29 @@
         scratch_shapes=[pltpu.SemaphoreType.DMA((devices,)), pltpu.SemaphoreType.DMA((devices,))],
         compiler_params=pltpu.CompilerParams(collective_id=0, has_side_effects=True),
     )(run)
-    run_keys = runs[:, :rows, :].reshape(devices, per_device)
-    samples = run_keys.reshape(devices, devices, spacing)[:, :, spacing - 1].reshape(-1)
-    order = lax.iota(jnp.int32, devices * devices)
-    beneath = samples[:, None] < samples[None, :] + (order[:, None] < order[None, :]).astype(jnp.int32)
-    ranks = jnp.sum(beneath.astype(jnp.int32), axis=0)
-    index = lax.iota(jnp.int32, per_device)[None, :]
-    run_of = lax.iota(jnp.int32, devices)[:, None]
-
-    def reach(j):
-        chosen = ranks == j * devices - 1
-        key = jnp.sum(jnp.where(chosen, samples, 0))
-        which = jnp.sum(jnp.where(chosen, order, 0))
-        sample_run, sample_index = which // devices, (which % devices) * spacing + spacing - 1
-        ahead = (run_of < sample_run) | (run_of == sample_run) & (index <= sample_index)
-        count = jnp.sum((run_keys < key + ahead.astype(jnp.int32)).astype(jnp.int32), axis=1)
-        return jnp.where(j == 0, 0, jnp.where(j == devices, per_device, count))
-
-    low, high = reach(me), reach(me + 1)
-    each = lax.iota(jnp.int32, devices)
-    stop = jnp.sum(jnp.where(each[:, None] <= each[None, :], (high - low)[:, None], 0), axis=0)
-    start = stop - (high - low)
-    sorted_keys, sorted_payloads, digest = pl.pallas_call(
-        functools.partial(bucket_kernel, devices, rows),
+    many = LANES // spacing
+    blocks = devices * rows // LANES
+    sorted_keys, sorted_payloads, size, digest = pl.pallas_call(
+        functools.partial(bucket_kernel, devices, rows, spacing),
         out_shape=(
             jax.ShapeDtypeStruct((2 * rows, LANES), jnp.int32),
             jax.ShapeDtypeStruct((2 * rows, LANES), jnp.int32),
             jax.ShapeDtypeStruct((1,), jnp.int32),
+            jax.ShapeDtypeStruct((1,), jnp.int32),
         ),
-        in_specs=[smem] * 3 + [vmem],
-        out_specs=(vmem, vmem, smem),
+        in_specs=[vmem],
+        out_specs=(vmem, vmem, smem, smem),
         scratch_shapes=[
             pltpu.VMEM((12 * rows, 2 * per_device), jnp.bfloat16),
             pltpu.VMEM((LANES, 2 * per_device), jnp.bfloat16),
+            pltpu.VMEM((blocks, many, LANES), jnp.int32),
+            pltpu.VMEM((devices * rows, LANES), jnp.int32),
+            pltpu.VMEM((blocks * many, 8, LANES), jnp.int32),
+            pltpu.VMEM((devices, LANES), jnp.int32),
+            pltpu.VMEM((devices, LANES), jnp.int32),
+            pltpu.VMEM((devices, LANES), jnp.int32),
         ],
-    )(low, start, stop, runs)
-    size = stop[devices - 1].reshape(1)
+    )(runs)
     return (sorted_keys.reshape(-1)[:bucket_cap], sorted_payloads.reshape(-1)[:bucket_cap], size, digest)
 
 

time: 37.6 us -> 24.6 us (0.65)
  other arithmetic: 5.67 us -> 0 us
  between operations: 5.97 us -> 0.64 us
  local copies, waits for them, and re-layouts: 3.05 us -> 0 us
  Pallas kernels: 22.5 us -> 23.7 us
    reduce_sum x5 -> x0, other arithmetic: 4.59 us -> none  [the longest x1 2.66 us: reach(): jnp.sum((run_keys < key + ahead.astype(jnp.int32)).astype(jnp.int32), axi...]
    slice x3 -> x0, local copies, waits for them, and re-layouts: 2.36 us -> none  [the longest x1 1.25 us: body(): size = stop[devices - 1].reshape(1)]
    pallas_call x1, Pallas kernels: 4.28 us -> 5.4 us  [body(): pl.pallas_call(functools.partial(bucket_kernel, devices, rows, spacing),...]
    sub x2 -> x0, other arithmetic: 1.06 us -> none  [the longest x1 0.54 us: body(): start = stop - (high - low)]
where the time goes in v2:
time: 24.6 us; the launch traced here: 24.3 us
  Pallas kernels  23.7 us (96%)
  between operations  0.64 us (3%)
    pallas_call x1, Pallas kernels, body(): pl.pallas_call(functools.partial(gather_kernel, devices, inner), out_shap...  16.1 us
    pallas_call x1, Pallas kernels, body(): pl.pallas_call(functools.partial(bucket_kernel, devices, rows, spacing),...  5.4 us
    pallas_call x1, Pallas kernels, body(): pl.pallas_call(functools.partial(local_kernel, rows), out_shape=jax.Shape...  2.14 us

profile of v2, /device:TPU:0, one launch (start us, length us, event | category | flops | bytes accessed | tf_op | source)
XLA Modules:
  0.0 24.3 jit_solution(4616055557656459024)
XLA Ops:
  0.6 2.1 %shard_map.57.run_ref = s32[16,128]{1,0:T(8,128)} custom-call(s32[8,128]{1,0:T(8,128)} %bitcast.6, s32[8,128]{1,0:T(8,128)} %bitcast.7), custom_call_target="tpu_custom_call" | custom-call | tf_op jit(solution)/shard_map/pallas_call | solution.py:248
  2.8 16.1 %shard_map.58.all_ref = s32[32,16,128]{2,1,0:T(8,128)} custom-call(s32[16,128]{1,0:T(8,128)} %shard_map.57.run_ref), custom_call_target="tpu_custom_call" | custom-call | tf_op jit(solution)/shard_map/pallas_call | solution.py:258
  18.9 5.4 %shard_map.59 = (s32[16,128]{1,0:T(8,128)}, s32[16,128]{1,0:T(8,128)}, s32[1]{0:T(128)}, s32[1]{0:T(128)}) custom-call(s32[32,16,128]{2,1,0:T(8,128)} %shard_map.58.all_ref), custom_call_target="tpu_custom_call" | custom-call | tf_op jit(solution)/shard_map/pallas_call | solution.py:268

commit v3 on v2

--- a/solution.py
+++ b/solution.py
@@ -56,51 +56,85 @@
     return key.astype(jnp.int32), value.astype(jnp.int32)
 
 
-def local_kernel(rows, key_ref, value_ref, run_ref, left_ref, right_ref):
-    keys, values = key_ref[...], value_ref[...]
+def gather_kernel(
+    devices, inner, rows, key_in, value_in, all_ref, left_ref, right_ref, run_ref, send_sem, recv_sem, pass_sem
+):
+    gx, gy = lax.axis_index("gx"), lax.axis_index("gy")
+    me = gx * inner + gy
+    core = lax.rem(gx, 2)
+    across = 1 - 2 * core
+    partner = (gx + across, gy)
+    chips = devices // 2
+    chip = gx // 2 * inner + gy
+
+    def place(c):
+        return (c // inner * 2 + core, lax.rem(c, inner))
+
+    def owner(k):
+        x, y = place(lax.rem(chip + chips - k, chips))
+        return x * inner + y
+
+    barrier = pltpu.get_barrier_semaphore()
+
+    @pl.loop(1, chips)
+    def _(k):
+        pl.semaphore_signal(barrier, inc=1, device_id=place(lax.rem(chip + k, chips)), device_id_type=MESH)
+
+    pl.semaphore_signal(barrier, inc=1, device_id=partner, device_id_type=MESH)
+
+    keys, values = key_in[...], value_in[...]
     ranks = rank_rows(keys, rows)
     key, value = place_rows(ranks, keys, values, rows, left_ref, right_ref)
     run_ref[:rows, :] = key
     run_ref[rows:, :] = value
-
-
-def gather_kernel(devices, inner, run_ref, all_ref, send_sem, recv_sem):
-    me = lax.axis_index(("gx", "gy"))
-
-    def place(other):
-        return (other // inner, lax.rem(other, inner))
-
-    barrier = pltpu.get_barrier_semaphore()
-
-    @pl.loop(1, devices)
-    def _(k):
-        pl.semaphore_signal(barrier, inc=1, device_id=place(lax.rem(me + k, devices)), device_id_type=MESH)
-
-    pl.semaphore_wait(barrier, devices - 1)
-
-    def copy(k, owner):
+    all_ref[me, :rows, :] = key
+    all_ref[me, rows:, :] = value
+
+    pl.semaphore_wait(barrier, chips)
+
+    def send(k, source):
         return pltpu.make_async_remote_copy(
             src_ref=run_ref,
-            dst_ref=all_ref.at[owner],
+            dst_ref=all_ref.at[source],
             send_sem=send_sem.at[k],
-            recv_sem=recv_sem.at[owner],
-            device_id=place(lax.rem(me + k, devices)),
+            recv_sem=recv_sem.at[source],
+            device_id=place(lax.rem(chip + k, chips)),
             device_id_type=MESH,
         )
 
-    @pl.loop(1, devices)
-    def _(k):
-        copy(k, me).start()
-
-    all_ref[me] = run_ref[...]
-
-    @pl.loop(1, devices)
-    def _(k):
-        copy(k, lax.rem(me + devices - k, devices)).wait_recv()
-
-    @pl.loop(1, devices)
-    def _(k):
-        copy(k, me).wait_send()
+    def pass_on(k, source, block):
+        return pltpu.make_async_remote_copy(
+            src_ref=block,
+            dst_ref=all_ref.at[source],
+            send_sem=pass_sem.at[k],
+            recv_sem=recv_sem.at[source],
+            device_id=partner,
+            device_id_type=MESH,
+        )
+
+    @pl.loop(1, chips)
+    def _(k):
+        send(k, me).start()
+
+    pass_on(0, me, run_ref).start()
+
+    @pl.loop(1, chips)
+    def _(k):
+        source = owner(k)
+        send(k, source).wait_recv()
+        pass_on(k, source, all_ref.at[source]).start()
+
+    @pl.loop(0, chips)
+    def _(k):
+        pass_on(k, owner(k) + across * inner, run_ref).wait_recv()
+
+    @pl.loop(1, chips)
+    def _(k):
+        send(k, me).wait_send()
+
+    @pl.loop(0, chips)
+    def _(k):
+        pass_on(k, me, run_ref).wait_send()
 
 
 def dot(left, right):
@@ -245,24 +279,21 @@
     rows = per_device // LANES
     vmem = pl.BlockSpec(memory_space=pltpu.VMEM)
     smem = pl.BlockSpec(memory_space=pltpu.SMEM)
-    run = pl.pallas_call(
-        functools.partial(local_kernel, rows),
-        out_shape=jax.ShapeDtypeStruct((2 * rows, LANES), jnp.int32),
+    runs = pl.pallas_call(
+        functools.partial(gather_kernel, devices, inner, rows),
+        out_shape=jax.ShapeDtypeStruct((devices, 2 * rows, LANES), jnp.int32),
         in_specs=[vmem] * 2,
         out_specs=vmem,
         scratch_shapes=[
             pltpu.VMEM((6 * rows, per_device), jnp.bfloat16),
             pltpu.VMEM((LANES, per_device), jnp.bfloat16),
+            pltpu.VMEM((2 * rows, LANES), jnp.int32),
+            pltpu.SemaphoreType.DMA((devices // 2,)),
+            pltpu.SemaphoreType.DMA((devices,)),
+            pltpu.SemaphoreType.DMA((devices // 2,)),
         ],
+        compiler_params=pltpu.CompilerParams(collective_id=0, has_side_effects=True),
     )(record_keys.reshape(rows, LANES), payloads.reshape(rows, LANES))
-    runs = pl.pallas_call(
-        functools.partial(gather_kernel, devices, inner),
-        out_shape=jax.ShapeDtypeStruct((devices, 2 * rows, LANES), jnp.int32),
-        in_specs=[vmem],
-        out_specs=vmem,
-        scratch_shapes=[pltpu.SemaphoreType.DMA((devices,)), pltpu.SemaphoreType.DMA((devices,))],
-        compiler_params=pltpu.CompilerParams(collective_id=0, has_side_effects=True),
-    )(run)
     many = LANES // spacing
     blocks = devices * rows // LANES
     sorted_keys, sorted_payloads, size, digest = pl.pallas_call(

time: 24.6 us -> 19.8 us (0.80)
  Pallas kernels: 23.7 us -> 18.9 us
    pallas_call x2 -> x1, Pallas kernels: 18.3 us -> 13.5 us  [body(): pl.pallas_call(functools.partial(gather_kernel, devices, inner, rows), ou...]
where the time goes in v3:
time: 19.8 us; the launch traced here: 19.5 us
  Pallas kernels  18.9 us (95%)
  between operations  0.64 us (3%)
    pallas_call x1, Pallas kernels, body(): pl.pallas_call(functools.partial(gather_kernel, devices, inner, rows), ou...  13.5 us
    pallas_call x1, Pallas kernels, body(): pl.pallas_call(functools.partial(bucket_kernel, devices, rows, spacing),...  5.4 us

profile of v3, /device:TPU:0, one launch (start us, length us, event | category | flops | bytes accessed | tf_op | source)
XLA Modules:
  0.0 19.5 jit_solution(11154734290370968953)
XLA Ops:
  0.6 13.5 %shard_map.57.all_ref = s32[32,16,128]{2,1,0:T(8,128)} custom-call(s32[8,128]{1,0:T(8,128)} %bitcast.6, s32[8,128]{1,0:T(8,128)} %bitcast.7), custom_call_target="tpu_custom_call" | custom-call | tf_op jit(solution)/shard_map/pallas_call | solution.py:282
  14.1 5.4 %shard_map.58 = (s32[16,128]{1,0:T(8,128)}, s32[16,128]{1,0:T(8,128)}, s32[1]{0:T(128)}, s32[1]{0:T(128)}) custom-call(s32[32,16,128]{2,1,0:T(8,128)} %shard_map.57.all_ref), custom_call_target="tpu_custom_call" | custom-call | tf_op jit(solution)/shard_map/pallas_call | solution.py:299

commit v4 on v3

--- a/solution.py
+++ b/solution.py
@@ -137,6 +137,73 @@
         pass_on(k, me, run_ref).wait_send()
 
 
+def rank_filled(keys, size, shells, count_ref):
+    turned = keys.T
+    sub = lax.broadcasted_iota(jnp.int32, (LANES, LANES), 0)
+    lane = lax.broadcasted_iota(jnp.int32, (LANES, LANES), 1)
+    earlier = (sub < lane).astype(jnp.int32)
+    count_ref[...] = jnp.zeros_like(count_ref)
+
+    def shell(begin, end):
+        counts = [jnp.zeros((8, LANES), jnp.int32) for _ in range(end)]
+        for c in range(end):
+            column = jnp.broadcast_to(turned[:, c : c + 1], (LANES, LANES))
+            for b in range(begin if c < begin else 0, end):
+                row = keys[b : b + 1, :]
+                if c < b:
+                    below = column <= row
+                elif c > b:
+                    below = column < row
+                else:
+                    below = column < row + earlier
+                counts[b] = counts[b] + jnp.sum(below.astype(jnp.int32).reshape(LANES // 8, 8, LANES), axis=0)
+        for b in range(end):
+            count_ref[b] += counts[b]
+
+    for begin, end in shells:
+        if begin == 0:
+            shell(begin, end)
+        else:
+            pl.when(size > begin * LANES)(functools.partial(shell, begin, end))
+
+
+def place_filled(keys, values, size, rows, shells, count_ref, left_ref, right_ref, moved_ref):
+    sub = lax.broadcasted_iota(jnp.int32, (LANES, LANES), 0)
+    high = lax.broadcasted_iota(jnp.int32, (rows, LANES), 0)
+
+    def shell(begin, end):
+        for b in range(begin, end):
+            rank = jnp.sum(count_ref[b], axis=0, keepdims=True)
+            at = slice(b * LANES, (b + 1) * LANES)
+            right_ref[:, at] = (sub == (rank & (LANES - 1))).astype(jnp.float32).astype(jnp.bfloat16)
+            mine = high == (rank >> 7)
+            pieces = []
+            for array in (keys, values):
+                row = array[b : b + 1, :]
+                for shift in (0, 8, 16):
+                    byte = ((row >> shift) & 255).astype(jnp.float32)
+                    pieces.append(jnp.where(mine, byte, 0.0))
+            left_ref[:, at] = jnp.concatenate(pieces, axis=0).astype(jnp.bfloat16)
+        at = slice(begin * LANES, end * LANES)
+        moved = lax.dot_general(
+            left_ref[:, at], right_ref[:, at], (((1,), (1,)), ((), ())), preferred_element_type=jnp.float32
+        )
+        if begin == 0:
+            moved_ref[...] = moved
+        else:
+            moved_ref[...] += moved
+
+    for begin, end in shells:
+        if begin == 0:
+            shell(begin, end)
+        else:
+            pl.when(size > begin * LANES)(functools.partial(shell, begin, end))
+    part = [moved_ref[i * rows : (i + 1) * rows, :] for i in range(6)]
+    key = part[0] + 256.0 * part[1] + 65536.0 * part[2]
+    value = part[3] + 256.0 * part[4] + 65536.0 * part[5]
+    return key.astype(jnp.int32), value.astype(jnp.int32)
+
+
 def dot(left, right):
     return jnp.dot(
         left.astype(jnp.float32).astype(jnp.bfloat16),
@@ -206,7 +273,7 @@
 
 def bucket_kernel(
     devices, rows, spacing, all_ref, key_ref, value_ref, size_ref, digest_ref,
-    left_ref, right_ref, turned_ref, keys_ref, count_ref, lows_ref, starts_ref, stops_ref,
+    left_ref, right_ref, turned_ref, keys_ref, count_ref, lows_ref, starts_ref, stops_ref, tally_ref, moved_ref,
 ):
     me = lax.axis_index(("gx", "gy"))
     span = rows * LANES
@@ -257,18 +324,20 @@
     none = jnp.zeros((rows, LANES), jnp.int32)
     k0, k1, v0, v1 = lax.fori_loop(0, devices, take, (empty, empty, none, none), unroll=8)
     held_keys, held_values = jnp.concatenate([k0, k1], axis=0), jnp.concatenate([v0, v1], axis=0)
-    ranks = rank_rows(held_keys, 2 * rows)
-    key, value = place_rows(ranks, held_keys, held_values, 2 * rows, left_ref, right_ref)
+    size = jnp.max(stops_ref[devices - 1 :, :])
+    edges = (0, rows, rows + rows // 8, rows + rows // 4, rows + rows // 2, 2 * rows)
+    shells = tuple(zip(edges[:-1], edges[1:]))
+    rank_filled(held_keys, size, shells, tally_ref)
+    key, value = place_filled(held_keys, held_values, size, 2 * rows, shells, tally_ref, left_ref, right_ref, moved_ref)
     rank = lax.broadcasted_iota(jnp.int32, (2 * rows, LANES), 0) * LANES + lax.broadcasted_iota(
         jnp.int32, (2 * rows, LANES), 1
     )
-    size = stops_ref[devices - 1 :, :]
     filled = rank < size
     key_ref[...] = jnp.where(filled, key, -1)
     value_ref[...] = jnp.where(filled, value, -1)
     mixed = (key + 3 * value + 5 * rank) & 1023
     digest_ref[0] = jnp.sum(jnp.where(filled, 2 * mixed - 1023, 0))
-    size_ref[0] = jnp.max(size)
+    size_ref[0] = size
 
 
 def body(inner, record_keys, payloads):
@@ -281,7 +350,7 @@
     smem = pl.BlockSpec(memory_space=pltpu.SMEM)
     runs = pl.pallas_call(
         functools.partial(gather_kernel, devices, inner, rows),
-        out_shape=jax.ShapeDtypeStruct((devices, 2 * rows, LANES), jnp.int32),
+        out_shape=pltpu.VMEM((devices, 2 * rows, LANES), jnp.int32),
         in_specs=[vmem] * 2,
         out_specs=vmem,
         scratch_shapes=[
@@ -315,8 +384,10 @@
             pltpu.VMEM((devices, LANES), jnp.int32),
             pltpu.VMEM((devices, LANES), jnp.int32),
             pltpu.VMEM((devices, LANES), jnp.int32),
+            pltpu.VMEM((2 * rows, 8, LANES), jnp.int32),
+            pltpu.VMEM((12 * rows, LANES), jnp.float32),
         ],
-    )(runs)
+    )(pltpu.with_memory_space_constraint(runs, pltpu.VMEM))
     return (sorted_keys.reshape(-1)[:bucket_cap], sorted_payloads.reshape(-1)[:bucket_cap], size, digest)
 
 

time: 19.8 us -> 17.8 us (0.90)
  Pallas kernels: 18.9 us -> 17 us
    pallas_call x1, Pallas kernels: 5.4 us -> 4.2 us  [body(): pl.pallas_call(functools.partial(bucket_kernel, devices, rows, spacing),...]
    pallas_call x1, Pallas kernels: 13.5 us -> 12.8 us  [body(): pl.pallas_call(functools.partial(gather_kernel, devices, inner, rows), ou...]
where the time goes in v4:
time: 17.8 us; the launch traced here: 17.7 us
  Pallas kernels  17 us (96%)
  between operations  0.64 us (4%)
    pallas_call x1, Pallas kernels, body(): pl.pallas_call(functools.partial(gather_kernel, devices, inner, rows), ou...  12.8 us
    pallas_call x1, Pallas kernels, body(): pl.pallas_call(functools.partial(bucket_kernel, devices, rows, spacing),...  4.2 us

profile of v4, /device:TPU:0, one launch (start us, length us, event | category | flops | bytes accessed | tf_op | source)
XLA Modules:
  0.0 17.7 jit_solution(12231415415986661122)
XLA Ops:
  0.6 12.8 %shard_map.57.all_ref = s32[32,16,128]{2,1,0:T(8,128)S(1)} custom-call(s32[8,128]{1,0:T(8,128)} %bitcast.6, s32[8,128]{1,0:T(8,128)} %bitcast.7), custom_call_target="tpu_custom_call" | custom-call | tf_op jit(solution)/shard_map/pallas_call | solution.py:351
  13.5 4.2 %shard_map.58 = (s32[16,128]{1,0:T(8,128)}, s32[16,128]{1,0:T(8,128)}, s32[1]{0:T(128)}, s32[1]{0:T(128)}) custom-call(s32[32,16,128]{2,1,0:T(8,128)S(1)} %shard_map.57.all_ref), custom_call_target="tpu_custom_call" | custom-call | tf_op jit(solution)/shard_map/pallas_call | solution.py:368

commit v5 on v4

--- a/solution.py
+++ b/solution.py
@@ -85,10 +85,14 @@
     keys, values = key_in[...], value_in[...]
     ranks = rank_rows(keys, rows)
     key, value = place_rows(ranks, keys, values, rows, left_ref, right_ref)
-    run_ref[:rows, :] = key
-    run_ref[rows:, :] = value
-    all_ref[me, :rows, :] = key
-    all_ref[me, rows:, :] = value
+    half = rows // 2
+    low = value | ((key & 255) << 24)
+    top = key >> 8
+    high = top[:half, :] | (top[half:, :] << 16)
+    run_ref[:rows, :] = low
+    run_ref[rows:, :] = high
+    all_ref[me, :rows, :] = low
+    all_ref[me, rows:, :] = high
 
     pl.semaphore_wait(barrier, chips)
 
@@ -282,7 +286,10 @@
     sub = lax.broadcasted_iota(jnp.int32, (rows, LANES), 0)
     spot = sub * LANES + lane
 
-    keys = all_ref[:, :rows, :].reshape(height, LANES)
+    low_word = all_ref[:, :rows, :]
+    high_word = all_ref[:, rows:, :]
+    tops = jnp.concatenate([high_word & 65535, lax.shift_right_logical(high_word, 16)], axis=1)
+    keys = ((tops << 8) | lax.shift_right_logical(low_word, 24)).reshape(height, LANES)
     low, high = splitter_pair(devices, spacing, me, keys, turned_ref, keys_ref, count_ref)
     flat = lax.broadcasted_iota(jnp.int32, (height, LANES), 0) * LANES + lax.broadcasted_iota(
         jnp.int32, (height, LANES), 1
@@ -310,7 +317,7 @@
             x = jnp.take_along_axis(x, from_lane, axis=1)
             return jnp.take_along_axis(x, from_row, axis=0)
 
-        k, v = rotate(all_ref[r, :rows, :]), rotate(all_ref[r, rows:, :])
+        k, v = rotate(keys_ref[pl.ds(r * rows, rows), :]), rotate(all_ref[r, :rows, :] & 16777215)
         first = (spot >= start) & (spot < stop)
         second = (spot + span >= start) & (spot + span < stop)
         return (
@@ -350,13 +357,13 @@
     smem = pl.BlockSpec(memory_space=pltpu.SMEM)
     runs = pl.pallas_call(
         functools.partial(gather_kernel, devices, inner, rows),
-        out_shape=pltpu.VMEM((devices, 2 * rows, LANES), jnp.int32),
+        out_shape=pltpu.VMEM((devices, rows + rows // 2, LANES), jnp.int32),
         in_specs=[vmem] * 2,
         out_specs=vmem,
         scratch_shapes=[
             pltpu.VMEM((6 * rows, per_device), jnp.bfloat16),
             pltpu.VMEM((LANES, per_device), jnp.bfloat16),
-            pltpu.VMEM((2 * rows, LANES), jnp.int32),
+            pltpu.VMEM((rows + rows // 2, LANES), jnp.int32),
             pltpu.SemaphoreType.DMA((devices // 2,)),
             pltpu.SemaphoreType.DMA((devices,)),
             pltpu.SemaphoreType.DMA((devices // 2,)),

time: 17.8 us -> 17.1 us (0.961)
  Pallas kernels: 17 us -> 16.3 us
    pallas_call x1, Pallas kernels: 12.8 us -> 12.1 us  [body(): pl.pallas_call(functools.partial(gather_kernel, devices, inner, rows), ou...]
where the time goes in v5:
time: 17.1 us; the launch traced here: 17 us
  Pallas kernels  16.3 us (95%)
  between operations  0.64 us (4%)
    pallas_call x1, Pallas kernels, body(): pl.pallas_call(functools.partial(gather_kernel, devices, inner, rows), ou...  12.1 us
    pallas_call x1, Pallas kernels, body(): pl.pallas_call(functools.partial(bucket_kernel, devices, rows, spacing),...  4.21 us

profile of v5, /device:TPU:0, one launch (start us, length us, event | category | flops | bytes accessed | tf_op | source)
XLA Modules:
  0.0 17.0 jit_solution(7046792253477618235)
XLA Ops:
  0.6 12.1 %shard_map.57.all_ref = s32[32,12,128]{2,1,0:T(8,128)S(1)} custom-call(s32[8,128]{1,0:T(8,128)} %bitcast.6, s32[8,128]{1,0:T(8,128)} %bitcast.7), custom_call_target="tpu_custom_call" | custom-call | tf_op jit(solution)/shard_map/pallas_call | solution.py:358
  12.7 4.2 %shard_map.58 = (s32[16,128]{1,0:T(8,128)}, s32[16,128]{1,0:T(8,128)}, s32[1]{0:T(128)}, s32[1]{0:T(128)}) custom-call(s32[32,12,128]{2,1,0:T(8,128)S(1)} %shard_map.57.all_ref), custom_call_target="tpu_custom_call" | custom-call | tf_op jit(solution)/shard_map/pallas_call | solution.py:375
